TPU v7x, 128 devices: a whole 4x4x4 slice. The times are simulated.
128 devices in a mesh: dp: 16 (over x_lo, z, core), expert: 8 (over y, x_hi).
Axes of the slice: x: 4 (x_hi: 2, x_lo: 2; x = x_hi * 2 + x_lo), y: 4, z: 4, core: 2. Of those that a mesh axis runs over, the one named last changes fastest.
Arguments:
- tokens: bfloat16 [16384, 2048], P(('dp', 'expert')), may hold values from -6 to 6
- norm_gain: float32 [2048], replicated, may hold values from 0.25 to 1.75
- router_weight: bfloat16 [2048, 64], P('dp'), may hold values from -0.25 to 0.25
- expert_ids: int32 [16384, 8], P(('dp', 'expert')), may hold values from 0 to 63, all different within a row; in each aligned block of 128 rows (0 to 127, 128 to 255, ...) at most 32 rows name the same one
- gate_weight: bfloat16 [8, 2048, 1024], P('expert', 'dp'), may hold values from -0.125 to 0.125
- up_weight: bfloat16 [8, 2048, 1024], P('expert', 'dp'), may hold values from -0.125 to 0.125
- down_weight: bfloat16 [8, 2048, 1024], P('expert', 'dp'), may hold values from -0.1875 to 0.1875
- cotangent: bfloat16 [16384, 2048], P(('dp', 'expert')), may hold values from -6 to 6
Outputs:
- mixed: bfloat16 [16384, 2048], P(('dp', 'expert'))
- d_tokens: bfloat16 [16384, 2048], P(('dp', 'expert'))
- d_gain: float32 [2048], replicated
- d_router: float32 [2048, 64], P('dp')
- d_gate: bfloat16 [8, 2048, 1024], P('expert', 'dp')
- d_up: bfloat16 [8, 2048, 1024], P('expert', 'dp')
- d_down: bfloat16 [8, 2048, 1024], P('expert', 'dp')
Inputs may be any that keep to these rules, and one draw needn't show every extreme that they name: `expert_ids`: each row names 8 different experts; in the rows of one device no expert is named more than 32 times.
All inputs are finite; a program needn't handle non-finite values.
Results may differ from a plain program's by a relative error of at most 0.018.
Values may be sent and summed in bfloat16 or wider, within the bound.
No kernel may reach another device: no remote copies, remote signals or barrier semaphores. Data moves between devices by JAX's collectives and lax.ppermute only.
A program may use at most 128 MiB of HBM per device.

v0:
```python
import jax
import jax.numpy as jnp
from jax import lax
from jax.sharding import PartitionSpec as P

D = 2048
FF = 1024
CAP = 32
EPSILON = 1e-05
HIGHEST = lax.Precision.HIGHEST


def in_one_piece(arrays, axis, dim, along):
    both = jnp.concatenate(arrays, axis=along)
    result, at, finished = (lax.all_gather(both, axis, axis=dim, tiled=True), 0, [])
    for a in arrays:
        finished.append(lax.slice_in_dim(result, at, at + a.shape[along], axis=along))
        at += a.shape[along]
    return tuple(finished)


def split_up(x, dim, length):
    shape = x.shape
    pieces = x.reshape(*shape[:dim], length, shape[dim] // length, *shape[dim + 1 :])
    return jnp.moveaxis(pieces, dim, 0)


def sum_at_owner(x, axis, dim):
    length = lax.axis_size(axis)
    pieces = lax.all_to_all(split_up(x, dim, length), axis, 0, 0, tiled=True)
    return jnp.sum(pieces.astype(jnp.float32), axis=0)


def copy_for_each(x, axis):
    copies = jnp.broadcast_to(x, (lax.axis_size(axis), *x.shape))
    return lax.all_to_all(copies, axis, split_axis=0, concat_axis=0, tiled=True)


def over_copies(x, axis):
    everything = copy_for_each(x, axis)
    return jnp.sum(everything.astype(jnp.float32), axis=0)


def normalize(inputs, norm_gain):
    meansq = jnp.mean(inputs * inputs, axis=-1, keepdims=True)
    return inputs * lax.rsqrt(meansq + EPSILON) * norm_gain


def gate_weights(logits, expert_ids):
    member = (
        expert_ids[:, :, None] == jnp.arange(logits.shape[-1], dtype=jnp.int32)[None, None, :]
    ).astype(jnp.float32)
    picked = jnp.sum(member * logits[:, None, :], axis=-1)
    raised = jnp.exp(picked)
    return raised / jnp.sum(raised, axis=-1, keepdims=True)


def pick_matrix(expert_ids, window, capacity):
    flat_ids = expert_ids.reshape(-1)
    chosen = (flat_ids[:, None] == jnp.arange(window, dtype=jnp.int32)[None, :]).astype(jnp.int32)
    before = jnp.cumsum(chosen, axis=0, dtype=jnp.int32) - chosen
    position = jnp.sum(before * chosen, axis=-1)
    target = jnp.where(flat_ids < window, flat_ids * capacity + position, -1)
    columns = jnp.arange(window * capacity, dtype=jnp.int32)
    matrix = (target[:, None] == columns[None, :]).astype(jnp.float32)
    return matrix.reshape(expert_ids.shape[0], expert_ids.shape[1], window * capacity)


def expert_forward(slot_rows, w_gate, w_up, w_down):
    gate_pre = jnp.dot(slot_rows, w_gate, preferred_element_type=jnp.float32)
    up_pre = jnp.dot(slot_rows, w_up, preferred_element_type=jnp.float32)
    active = (gate_pre * jax.nn.sigmoid(gate_pre) * up_pre).astype(jnp.bfloat16)
    output = jnp.dot(active, w_down.T, preferred_element_type=jnp.float32).astype(jnp.bfloat16)
    return (output, gate_pre, up_pre)


def expert_backward(slot_grads, gate_pre, up_pre, w_gate, w_up, w_down):
    sigmoid_gate = jax.nn.sigmoid(gate_pre)
    active = (gate_pre * sigmoid_gate * up_pre).astype(jnp.bfloat16)
    back = jnp.dot(slot_grads, w_down, preferred_element_type=jnp.float32)
    grad_gate = (back * up_pre * sigmoid_gate * (1.0 + gate_pre * (1.0 - sigmoid_gate))).astype(
        jnp.bfloat16
    )
    grad_upper = (back * gate_pre * sigmoid_gate).astype(jnp.bfloat16)
    grad_rows = jnp.dot(grad_gate, w_gate.T, preferred_element_type=jnp.float32)
    grad_rows = (
        grad_rows + jnp.dot(grad_upper, w_up.T, preferred_element_type=jnp.float32)
    ).astype(jnp.bfloat16)
    return (grad_rows, active, grad_gate, grad_upper)


def body(
    tokens, norm_gain, router_weight, expert_ids, gate_weight, up_weight, down_weight, cotangent
):
    window = lax.axis_size("expert")
    slot_count = window * CAP
    router_full = lax.all_gather(router_weight, "dp", axis=0, tiled=True)
    inputs = tokens.astype(jnp.float32)
    hidden = normalize(inputs, norm_gain).astype(jnp.bfloat16)
    logits = jnp.dot(hidden, router_full, preferred_element_type=jnp.float32)
    weights, gate_back = jax.vjp(lambda values: gate_weights(values, expert_ids), logits)
    pick_table = pick_matrix(expert_ids, window, CAP)
    spread_half = jnp.sum(pick_table, axis=1).astype(jnp.bfloat16)
    blending = jnp.einsum("tks,tk->ts", pick_table, weights, precision=HIGHEST)
    outgoing = (
        jnp.dot(spread_half.T, hidden, preferred_element_type=jnp.float32)
        .astype(jnp.bfloat16)
        .reshape(window, CAP, D)
    )
    weights_full = in_one_piece((gate_weight, up_weight, down_weight), "dp", 1, 0)
    w_gate = weights_full[0][0]
    w_up = weights_full[1][0]
    w_down = weights_full[2][0]
    arrived_rows = lax.all_to_all(outgoing, "expert", split_axis=0, concat_axis=0, tiled=True)
    lead = arrived_rows.shape[0]
    middle = arrived_rows.shape[1]
    output, gate_pre, up_pre = expert_forward(arrived_rows.reshape(-1, D), w_gate, w_up, w_down)
    produced = output.reshape(lead, middle, D)
    gate_slots = gate_pre.reshape(lead, middle, FF)
    upper_slots = up_pre.reshape(lead, middle, FF)
    returned = lax.all_to_all(produced, "expert", split_axis=0, concat_axis=0, tiled=True).reshape(
        slot_count, D
    )
    returned_wide = returned.astype(jnp.float32)
    mixed_out = jnp.dot(blending, returned_wide, precision=HIGHEST).astype(jnp.bfloat16)
    gathered_cot = jnp.dot(spread_half.T, cotangent, preferred_element_type=jnp.float32)
    per_slot = jnp.sum(gathered_cot * returned_wide, axis=-1)
    grad_weights = jnp.einsum("tks,s->tk", pick_table, per_slot, precision=HIGHEST)
    grad_logits = gate_back(grad_weights)[0]
    outgoing_grad = (
        jnp.dot(blending.T, cotangent.astype(jnp.float32), precision=HIGHEST)
        .astype(jnp.bfloat16)
        .reshape(window, CAP, D)
    )
    arrived_grad = lax.all_to_all(outgoing_grad, "expert", split_axis=0, concat_axis=0, tiled=True)
    flat_rows = arrived_rows.reshape(-1, D)
    flat_grads = arrived_grad.reshape(-1, D)
    grad_rows, active, grad_gate, grad_upper = expert_backward(
        flat_grads, gate_slots.reshape(-1, FF), upper_slots.reshape(-1, FF), w_gate, w_up, w_down
    )
    grad_back = lax.all_to_all(
        grad_rows.reshape(window, CAP, D), "expert", split_axis=0, concat_axis=0, tiled=True
    ).reshape(slot_count, D)
    term_gate = jnp.dot(flat_rows.T, grad_gate, preferred_element_type=jnp.float32)
    term_upper = jnp.dot(flat_rows.T, grad_upper, preferred_element_type=jnp.float32)
    term_down = jnp.dot(flat_grads.T, active, preferred_element_type=jnp.float32)
    summed = lax.psum_scatter(
        jnp.concatenate([term_gate, term_upper, term_down], axis=1).astype(jnp.bfloat16),
        "dp",
        scatter_dimension=0,
        tiled=True,
    ).astype(jnp.float32)
    grad_hidden = jnp.dot(spread_half, grad_back, preferred_element_type=jnp.float32)
    grad_hidden = grad_hidden + jnp.dot(
        grad_logits, router_full.astype(jnp.float32).T, precision=HIGHEST
    )
    unused_value, norm_back = jax.vjp(normalize, inputs, norm_gain)
    grad_inputs, grad_gain = norm_back(grad_hidden)
    grad_router = jnp.dot(hidden.astype(jnp.float32).T, grad_logits, precision=HIGHEST)
    router_part = sum_at_owner(grad_router.astype(jnp.bfloat16), "dp", 0)
    router_mine = over_copies(router_part.astype(jnp.bfloat16), "expert").astype(jnp.float32)
    gain_sum = lax.psum(grad_gain, ("dp", "expert"))
    grad_gate_out = summed[:, :FF].astype(jnp.bfloat16)[None]
    grad_up_out = summed[:, FF : 2 * FF].astype(jnp.bfloat16)[None]
    grad_down_out = summed[:, 2 * FF :].astype(jnp.bfloat16)[None]
    return (
        mixed_out,
        grad_inputs.astype(jnp.bfloat16),
        gain_sum,
        router_mine,
        grad_gate_out,
        grad_up_out,
        grad_down_out,
    )


def solution(mesh):
    in_specs = (
        P(("dp", "expert"), None),
        P(),
        P("dp", None),
        P(("dp", "expert"), None),
        P("expert", "dp", None),
        P("expert", "dp", None),
        P("expert", "dp", None),
        P(("dp", "expert"), None),
    )
    out_specs = (
        P(("dp", "expert"), None),
        P(("dp", "expert"), None),
        P(),
        P("dp", None),
        P("expert", "dp", None),
        P("expert", "dp", None),
        P("expert", "dp", None),
    )
    return jax.shard_map(body, mesh=mesh, in_specs=in_specs, out_specs=out_specs, check_vma=False)
```

profile of v0, /device:TPU:1, one launch (start us, length us, event | category | flops | bytes accessed | tf_op | source)
XLA Modules:
  0.0 330.0 jit_solution(3319858266487233548)
XLA Ops:
  7.3 2.2 pad_maximum_fusion.1
  10.4 2.3 reduce-window.6
  14.6 1.2 fusion.16
  15.9 2.5 convolution_convert_fusion.3
  18.4 7.5 %all-to-all-start = ((bf16[8,32,2048]{2,1,0:T(8,128)(2,1)}), bf16[8,32,2048]{2,1,0:T(8,128)(2,1)S(1)}, u32[]{:S(2)}, u32[]{:S(2)}) async-start(bf16[8,32,2048]{2,1,0:T(8,128)(2,1)} %bitcast.3), calls=%async_computation | async-start | bytes 2097152 | tf_op jit(solution)/shard_map/all_to_all | solution.py:114
  25.9 41.0 %all_gather.6 = bf16[2048,64]{0,1:T(8,128)(2,1)S(1)} all-gather(bf16[128,64]{0,1:T(8,128)(2,1)S(1)} %copy-done.14), channel_id=1, replica_groups=mesh['dp'=16,'expert'=8] {'dp'}, dimensions={0}, use_global_device_ids=true | all-gather | bytes 278528 | tf_op jit(solution)/shard_map/all_gather | solution.py:97
  69.0 2.1 convolution_convert_fusion.4
  71.1 6.8 %all-to-all-start.2 = ((bf16[8,32,2048]{2,1,0:T(8,128)(2,1)}), bf16[8,32,2048]{2,1,0:T(8,128)(2,1)S(1)}, u32[]{:S(2)}, u32[]{:S(2)}) async-start(bf16[8,32,2048]{2,1,0:T(8,128)(2,1)} %bitcast.109), calls=%async_computation.2 | async-start | bytes 2097152 | tf_op jit(solution)/shard_map/all_to_all | solution.py:135
  78.1 30.4 %all-gather.2.cloned.1.call-done = bf16[3,2048,1024]{2,1,0:T(8,128)(2,1)} async-done(((bf16[3,128,1024]{2,1,0:T(8,128)(2,1)}), bf16[3,2048,1024]{2,1,0:T(8,128)(2,1)}) %all-gather.2.cloned.1.call-update) | async-done | bytes 12582928 | tf_op jit(solution)/shard_map/all_gather | solution.py:15
  108.5 4.4 %fusion.3 = f32[256,1024]{1,0:T(8,128)} fusion(bf16[256,2048]{1,0:T(8,128)(2,1)S(1)} %bitcast.100, bf16[3,2048,1024]{2,1,0:T(8,128)(2,1)} %all-gather.2.cloned.1.call-done), kind=kOutput, calls=%fused_computation.10 | convolution fusion | flops 1073741824 | bytes 6291456 | tf_op jit(solution)/shard_map/dot_general | solution.py:71
  112.9 4.4 %fusion.1 = f32[256,1024]{1,0:T(8,128)} fusion(bf16[256,2048]{1,0:T(8,128)(2,1)S(1)} %bitcast.101, bf16[3,2048,1024]{2,1,0:T(8,128)(2,1)} %all-gather.2.cloned.1.call-done), kind=kOutput, calls=%fused_computation.8 | convolution fusion | flops 1073741824 | bytes 6291456 | tf_op jit(solution)/shard_map/dot_general | solution.py:70
  117.3 4.4 %multiply_convert_fusion = (bf16[256,1024]{1,0:T(8,128)(2,1)S(1)}, bf16[256,1024]{1,0:T(8,128)(2,1)S(1)}, bf16[256,1024]{1,0:T(8,128)(2,1)S(1)}) fusion(f32[256,1024]{1,0:T(8,128)} %fusion.1, f32[256,1024]{1,0:T(8,128)} %fusion.3, bf16[256,2048]{1,0:T(8,128)(2,1)S(1)} %bitcast.104, bf16[3,2048,1024]{2,1,0:T(8,128)(2,1)} %all-gather.2.cloned.1.call-done), kind=kOutput, calls=%fused_computation.36 | convolution fusion | flops 1077936128 | bytes 8912896 | tf_op jit(solution)/shard_map/dot_general | solution.py:80
  121.7 1.3 convolution_convert_fusion
  123.1 1.3 convolution_convert_fusion.1
  124.4 1.3 convolution_convert_fusion.2
  125.7 21.2 %pad_maximum_fusion = bf16[2048,3072]{0,1:T(8,128)(2,1)} fusion(bf16[2048,1024]{0,1:T(8,128)(2,1)S(1)} %convolution_convert_fusion, bf16[2048,1024]{0,1:T(8,128)(2,1)S(1)} %convolution_convert_fusion.1, bf16[2048,1024]{0,1:T(8,128)(2,1)S(1)} %convolution_convert_fusion.2), kind=kLoop, calls=%fused_computation | loop fusion | flops 37748736 | bytes 25165824 | tf_op jit(solution)/shard_map/concatenate | solution.py:148
  146.9 16.6 %copy.68 = bf16[2048,3072]{1,0:T(8,128)(2,1)} copy(bf16[2048,3072]{0,1:T(8,128)(2,1)} %pad_maximum_fusion) | data formatting | bytes 25165824
  164.6 4.6 %fusion.8 = bf16[256,2048]{1,0:T(8,128)(2,1)} fusion(bf16[256,1024]{1,0:T(8,128)(2,1)S(1)} %copy-done.8, bf16[3,2048,1024]{2,1,0:T(8,128)(2,1)} %all-gather.2.cloned.1.call-done), kind=kOutput, calls=%fused_computation.17 | convolution fusion | flops 1074266112 | bytes 5767168 | tf_op jit(solution)/shard_map/dot_general | solution.py:73
  169.2 6.1 %all-to-all-start.1 = ((bf16[8,32,2048]{2,1,0:T(8,128)(2,1)}), bf16[8,32,2048]{2,1,0:T(8,128)(2,1)S(1)}, u32[]{:S(2)}, u32[]{:S(2)}) async-start(bf16[8,32,2048]{2,1,0:T(8,128)(2,1)} %bitcast.8), calls=%async_computation.1 | async-start | bytes 2097152 | tf_op jit(solution)/shard_map/all_to_all | solution.py:121
  175.3 3.5 %fusion = f32[256,2048]{1,0:T(8,128)S(1)} fusion(bf16[256,1024]{1,0:T(8,128)(2,1)S(1)} %copy-done.6, bf16[3,2048,1024]{2,1,0:T(8,128)(2,1)} %all-gather.2.cloned.1.call-done), kind=kOutput, calls=%fused_computation.7 | convolution fusion | flops 1073741824 | bytes 6815744 | tf_op jit(solution)/shard_map/dot_general | solution.py:85
  178.9 4.5 %fusion.7 = bf16[256,2048]{1,0:T(8,128)(2,1)} fusion(f32[256,2048]{1,0:T(8,128)S(1)} %fusion, bf16[256,1024]{1,0:T(8,128)(2,1)S(1)} %copy-done.4, bf16[3,2048,1024]{2,1,0:T(8,128)(2,1)} %all-gather.2.cloned.1.call-done), kind=kOutput, calls=%fused_computation.16 | convolution fusion | flops 1074790400 | bytes 7864320 | tf_op jit(solution)/shard_map/dot_general | solution.py:87
  183.4 14.9 %all-to-all-done.1 = bf16[8,32,2048]{2,1,0:T(8,128)(2,1)S(1)} async-done(((bf16[8,32,2048]{2,1,0:T(8,128)(2,1)}), bf16[8,32,2048]{2,1,0:T(8,128)(2,1)S(1)}, u32[]{:S(2)}, u32[]{:S(2)}) %all-to-all-start.1) | async-done | bytes 1048608 | tf_op jit(solution)/shard_map/all_to_all | solution.py:121
  198.3 3.6 %all-to-all-start.3 = ((bf16[8,32,2048]{2,1,0:T(8,128)(2,1)}), bf16[8,32,2048]{2,1,0:T(8,128)(2,1)S(1)}, u32[]{:S(2)}, u32[]{:S(2)}) async-start(bf16[8,32,2048]{2,1,0:T(8,128)(2,1)} %bitcast.110), calls=%async_computation.3 | async-start | bytes 2097152 | tf_op jit(solution)/shard_map/all_to_all | solution.py:141
  202.4 3.6 %fusion.18 = f32[1,128,8]{2,0,1:T(1,128)S(1)} fusion(f32[256,1,1]{0,1,2:T(1,128)S(1)} %bitcast.115, s32[128,8]{1,0:T(8,128)S(1)} %copy.59), kind=kOutput, calls=%fused_computation.42 | convolution fusion | flops 3407872 | bytes 9216 | tf_op jit(solution)/shard_map/tks,s->tk/dot_general | solution.py:128
  207.6 16.8 %all-to-all-done.3 = bf16[8,32,2048]{2,1,0:T(8,128)(2,1)S(1)} async-done(((bf16[8,32,2048]{2,1,0:T(8,128)(2,1)}), bf16[8,32,2048]{2,1,0:T(8,128)(2,1)S(1)}, u32[]{:S(2)}, u32[]{:S(2)}) %all-to-all-start.3) | async-done | bytes 1048608 | tf_op jit(solution)/shard_map/all_to_all | solution.py:141
  224.4 6.8 %all-to-all-start.4 = ((bf16[16,128,64]{1,2,0:T(8,128)(2,1)}), bf16[16,128,64]{1,2,0:T(8,128)(2,1)S(1)}, u32[]{:S(2)}, u32[]{:S(2)}) async-start(bf16[16,128,64]{1,2,0:T(8,128)(2,1)} %bitcast.98), calls=%async_computation.4 | async-start | bytes 524288 | tf_op jit(solution)/shard_map/all_to_all | solution.py:30
  231.5 1.9 fusion.14
  235.2 5.1 %all-to-all-done.4 = bf16[16,128,64]{1,2,0:T(8,128)(2,1)S(1)} async-done(((bf16[16,128,64]{1,2,0:T(8,128)(2,1)}), bf16[16,128,64]{1,2,0:T(8,128)(2,1)S(1)}, u32[]{:S(2)}, u32[]{:S(2)}) %all-to-all-start.4) | async-done | bytes 262176 | tf_op jit(solution)/shard_map/all_to_all | solution.py:30
  241.0 3.4 %all-to-all-start.5 = ((bf16[8,128,64]{1,2,0:T(8,128)(2,1)}), bf16[8,128,64]{1,2,0:T(8,128)(2,1)S(1)}, u32[]{:S(2)}, u32[]{:S(2)}) async-start(bf16[8,128,64]{1,2,0:T(8,128)(2,1)} %broadcast_in_dim.44), calls=%async_computation.5 | async-start | bytes 262144 | tf_op jit(solution)/shard_map/all_to_all | solution.py:36
  244.4 1.4 convolution_convert_fusion.5
  245.8 72.5 %psum.7 = f32[2048]{0:T(1024)} all-reduce(f32[2048]{0:T(1024)S(1)} %get-tuple-element.42), channel_id=1, replica_groups=mesh['dp'=16,'expert'=8] {'dp','expert'}, use_global_device_ids=true, to_apply=%region_12.13 | all-reduce | flops 2048 | bytes 16384 | tf_op jit(solution)/shard_map/psum | solution.py:162
  318.9 1.2 fusion.43
  (85 shorter events, 14.7 us)
Async XLA Ops:
  7.2 61.8 %copy-start = (bf16[128,2048]{1,0:T(8,128)(2,1)S(1)}, bf16[128,2048]{1,0:T(8,128)(2,1)}, u32[]{:S(2)}) copy-start(bf16[128,2048]{1,0:T(8,128)(2,1)} %param.15) | copy-start | bytes 1572868
  7.2 60.9 %copy-start.13 = (s32[128,8]{0,1:T(8,128)S(1)}, s32[128,8]{0,1:T(8,128)}, u32[]{:S(2)}) copy-start(s32[128,8]{0,1:T(8,128)} %param.11) | copy-start | bytes 12292
  7.2 60.5 %copy-start.1 = (bf16[128,2048]{1,0:T(8,128)(2,1)S(1)}, bf16[128,2048]{1,0:T(8,128)(2,1)}, u32[]{:S(2)}) copy-start(bf16[128,2048]{1,0:T(8,128)(2,1)} %param.8) | copy-start | bytes 1572868
  7.2 60.5 %copy-start.12 = (f32[2048]{0:T(1024)S(1)}, f32[2048]{0:T(1024)}, u32[]{:S(2)}) copy-start(f32[2048]{0:T(1024)} %param.9) | copy-start | bytes 24580
  7.2 18.7 %copy-start.14 = (bf16[128,64]{0,1:T(8,128)(2,1)S(1)}, bf16[128,64]{0,1:T(8,128)(2,1)}, u32[]{:S(2)}) copy-start(bf16[128,64]{0,1:T(8,128)(2,1)} %param.10) | copy-start | bytes 49156
  7.2 101.3 %all-gather.2.cloned.1.call-start = ((), (), s32[]{:S(2)}) async-start(), calls=%async_computation.7 | async-start | bytes 13369344 | tf_op jit(solution)/shard_map/all_gather | solution.py:15
  15.9 10.0 %copy-start.17 = (f32[128]{0:T(128)}, f32[128]{0:T(128)S(1)}, u32[]{:S(2)}) copy-start(f32[128]{0:T(128)S(1)} %fusion.16) | copy-start | bytes 1540
  15.9 190.3 %copy-start.15 = (f32[128]{0:T(128)}, f32[128]{0:T(128)S(1)}, u32[]{:S(2)}) copy-start(f32[128]{0:T(128)S(1)} %fusion.34) | copy-start | bytes 1540
  18.4 52.6 %all-to-all-start = ((bf16[8,32,2048]{2,1,0:T(8,128)(2,1)}), bf16[8,32,2048]{2,1,0:T(8,128)(2,1)S(1)}, u32[]{:S(2)}, u32[]{:S(2)}) async-start(bf16[8,32,2048]{2,1,0:T(8,128)(2,1)} %bitcast.3), calls=%async_computation | async-start | bytes 2097152 | tf_op jit(solution)/shard_map/all_to_all | solution.py:114
  67.0 0.7 copy-start.2
  69.0 2.1 copy-start.9
  71.1 46.3 %all-to-all-start.2 = ((bf16[8,32,2048]{2,1,0:T(8,128)(2,1)}), bf16[8,32,2048]{2,1,0:T(8,128)(2,1)S(1)}, u32[]{:S(2)}, u32[]{:S(2)}) async-start(bf16[8,32,2048]{2,1,0:T(8,128)(2,1)} %bitcast.109), calls=%async_computation.2 | async-start | bytes 2097152 | tf_op jit(solution)/shard_map/all_to_all | solution.py:135
  77.9 241.0 %reduce-scatter.4.cloned.1.call-start = ((), (), s32[]{:S(2)}) async-start(), calls=%async_computation.8 | async-start | bytes 13369344
  121.7 1.4 copy-start.7
  121.7 1.4 copy-start.3
  121.7 2.7 copy-start.5
  163.5 1.0 copy-start.8
  164.6 10.7 %copy-start.6 = (bf16[256,1024]{1,0:T(8,128)(2,1)S(1)}, bf16[256,1024]{1,0:T(8,128)(2,1)}, u32[]{:S(2)}) copy-start(bf16[256,1024]{1,0:T(8,128)(2,1)} %copy-done.5) | copy-start | bytes 1572868
  169.2 29.1 %all-to-all-start.1 = ((bf16[8,32,2048]{2,1,0:T(8,128)(2,1)}), bf16[8,32,2048]{2,1,0:T(8,128)(2,1)S(1)}, u32[]{:S(2)}, u32[]{:S(2)}) async-start(bf16[8,32,2048]{2,1,0:T(8,128)(2,1)} %bitcast.8), calls=%async_computation.1 | async-start | bytes 2097152 | tf_op jit(solution)/shard_map/all_to_all | solution.py:121
  175.3 3.5 %copy-start.4 = (bf16[256,1024]{1,0:T(8,128)(2,1)S(1)}, bf16[256,1024]{1,0:T(8,128)(2,1)}, u32[]{:S(2)}) copy-start(bf16[256,1024]{1,0:T(8,128)(2,1)} %copy-done.3) | copy-start | bytes 1572868
  198.3 26.1 %all-to-all-start.3 = ((bf16[8,32,2048]{2,1,0:T(8,128)(2,1)}), bf16[8,32,2048]{2,1,0:T(8,128)(2,1)S(1)}, u32[]{:S(2)}, u32[]{:S(2)}) async-start(bf16[8,32,2048]{2,1,0:T(8,128)(2,1)} %bitcast.110), calls=%async_computation.3 | async-start | bytes 2097152 | tf_op jit(solution)/shard_map/all_to_all | solution.py:141
  206.2 0.6 copy-start.11
  224.4 15.9 %all-to-all-start.4 = ((bf16[16,128,64]{1,2,0:T(8,128)(2,1)}), bf16[16,128,64]{1,2,0:T(8,128)(2,1)S(1)}, u32[]{:S(2)}, u32[]{:S(2)}) async-start(bf16[16,128,64]{1,2,0:T(8,128)(2,1)} %bitcast.98), calls=%async_computation.4 | async-start | bytes 524288 | tf_op jit(solution)/shard_map/all_to_all | solution.py:30
  231.2 2.9 copy-start.16
  231.5 12.9 %copy-start.10 = (f32[128,1,256]{2,1,0:T(1,128)S(1)}, f32[128,1,256]{2,1,0:T(1,128)}, u32[]{:S(2)}) copy-start(f32[128,1,256]{2,1,0:T(1,128)} %copy-done.9) | copy-start | bytes 393220
  241.0 77.3 %all-to-all-start.5 = ((bf16[8,128,64]{1,2,0:T(8,128)(2,1)}), bf16[8,128,64]{1,2,0:T(8,128)(2,1)S(1)}, u32[]{:S(2)}, u32[]{:S(2)}) async-start(bf16[8,128,64]{1,2,0:T(8,128)(2,1)} %broadcast_in_dim.44), calls=%async_computation.5 | async-start | bytes 262144 | tf_op jit(solution)/shard_map/all_to_all | solution.py:36
Sparse Core Ops, SparseCore 0:
  9.7 98.7 all-gather.1
  163.7 106.8 reduce-scatter.3
where the time goes:
time: 331 us; the launch traced here: 330 us
  blocking collectives  114 us (34%)
  waiting for transfers between devices  67.2 us (20%)
  matrix products  43.8 us (13%)
  starting transfers between devices  34.4 us (10%)
  other arithmetic  30.8 us (9%)
  local copies, waits for them, and re-layouts  25.9 us (8%)
  between operations  14.4 us (4%)
    psum x1, blocking collectives, body(): gain_sum = lax.psum(grad_gain, ('dp', 'expert'))  72.5 us
    all_gather x1, blocking collectives, body(): router_full = lax.all_gather(router_weight, 'dp', axis=0, tiled=True)  41 us
    all_gather x1, waiting for transfers between devices, in_one_piece(): lax.all_gather(both, axis, axis=dim, tiled=True)  30.4 us
    unnamed x44, local copies, waits for them, and re-layouts  22.4 us
    concatenate x1, other arithmetic, body(): jnp.concatenate([term_gate, term_upper, term_down], axis=1)  21.2 us
    all_to_all x1, waiting for transfers between devices, body(): lax.all_to_all(grad_rows.reshape(window, CAP, D), 'expert', split_axis=0,...  16.8 us
    all_to_all x1, waiting for transfers between devices, body(): lax.all_to_all(produced, 'expert', split_axis=0, concat_axis=0, tiled=True)  14.9 us
    all_to_all x1, starting transfers between devices, body(): lax.all_to_all(outgoing, 'expert', split_axis=0, concat_axis=0, tiled=True)  7.46 us
  transfers between devices with their start and end apart: 8, of which 4 were waited for; matrix products, arithmetic and copies ran while one was open for 14% of the time, Pallas kernels for 0%

commit v1 on v0

--- a/solution.py
+++ b/solution.py
@@ -159,7 +159,8 @@
     grad_router = jnp.dot(hidden.astype(jnp.float32).T, grad_logits, precision=HIGHEST)
     router_part = sum_at_owner(grad_router.astype(jnp.bfloat16), "dp", 0)
     router_mine = over_copies(router_part.astype(jnp.bfloat16), "expert").astype(jnp.float32)
-    gain_sum = lax.psum(grad_gain, ("dp", "expert"))
+    reached = lax.psum(grad_gain, "dp")
+    gain_sum = lax.psum(reached, "expert")
     grad_gate_out = summed[:, :FF].astype(jnp.bfloat16)[None]
     grad_up_out = summed[:, FF : 2 * FF].astype(jnp.bfloat16)[None]
     grad_down_out = summed[:, 2 * FF :].astype(jnp.bfloat16)[None]

time: 331 us -> 312 us (0.943); the launches traced: 330 us -> 307 us
  blocking collectives: 114 us -> 90.9 us
    psum x1 -> x2, blocking collectives: 72.5 us -> 49.8 us  [the longest x1 28.3 us: body(): reached = lax.psum(grad_gain, 'dp')]
  transfers between devices with their start and end apart: 8 -> 8, of which waited for: 4 -> 4; matrix products, arithmetic and copies ran while one was open for 14% -> 15% of each run, Pallas kernels for 0% -> 0%
where the time goes in v1:
time: 312 us; the launch traced here: 307 us
  blocking collectives  90.9 us (29%)
  waiting for transfers between devices  67.2 us (22%)
  matrix products  43.8 us (14%)
  starting transfers between devices  34.4 us (11%)
  other arithmetic  30.8 us (10%)
  local copies, waits for them, and re-layouts  25.9 us (8%)
  between operations  14.4 us (5%)
    all_gather x1, blocking collectives, body(): router_full = lax.all_gather(router_weight, 'dp', axis=0, tiled=True)  41 us
    all_gather x1, waiting for transfers between devices, in_one_piece(): lax.all_gather(both, axis, axis=dim, tiled=True)  30.4 us
    psum x1, blocking collectives, body(): reached = lax.psum(grad_gain, 'dp')  28.3 us
    unnamed x44, local copies, waits for them, and re-layouts  22.4 us
    psum x1, blocking collectives, body(): gain_sum = lax.psum(reached, 'expert')  21.5 us
    concatenate x1, other arithmetic, body(): jnp.concatenate([term_gate, term_upper, term_down], axis=1)  21.2 us
    all_to_all x1, waiting for transfers between devices, body(): lax.all_to_all(grad_rows.reshape(window, CAP, D), 'expert', split_axis=0,...  16.8 us
    all_to_all x1, waiting for transfers between devices, body(): lax.all_to_all(produced, 'expert', split_axis=0, concat_axis=0, tiled=True)  14.9 us
  transfers between devices with their start and end apart: 8, of which 4 were waited for; matrix products, arithmetic and copies ran while one was open for 15% of the time, Pallas kernels for 0%

profile of v1, /device:TPU:1, one launch (start us, length us, event | category | flops | bytes accessed | tf_op | source)
XLA Modules:
  0.0 307.3 jit_solution(17884822598062070000)
XLA Ops:
  7.3 2.2 pad_maximum_fusion.1
  10.4 2.3 reduce-window.6
  14.6 1.2 fusion.16
  15.9 2.5 convolution_convert_fusion.3
  18.4 7.5 %all-to-all-start = ((bf16[8,32,2048]{2,1,0:T(8,128)(2,1)}), bf16[8,32,2048]{2,1,0:T(8,128)(2,1)S(1)}, u32[]{:S(2)}, u32[]{:S(2)}) async-start(bf16[8,32,2048]{2,1,0:T(8,128)(2,1)} %bitcast.3), calls=%async_computation | async-start | bytes 2097152 | tf_op jit(solution)/shard_map/all_to_all | solution.py:114
  25.9 41.0 %all_gather.6 = bf16[2048,64]{0,1:T(8,128)(2,1)S(1)} all-gather(bf16[128,64]{0,1:T(8,128)(2,1)S(1)} %copy-done.14), channel_id=1, replica_groups=mesh['dp'=16,'expert'=8] {'dp'}, dimensions={0}, use_global_device_ids=true | all-gather | bytes 278528 | tf_op jit(solution)/shard_map/all_gather | solution.py:97
  69.0 2.1 convolution_convert_fusion.4
  71.1 6.8 %all-to-all-start.2 = ((bf16[8,32,2048]{2,1,0:T(8,128)(2,1)}), bf16[8,32,2048]{2,1,0:T(8,128)(2,1)S(1)}, u32[]{:S(2)}, u32[]{:S(2)}) async-start(bf16[8,32,2048]{2,1,0:T(8,128)(2,1)} %bitcast.109), calls=%async_computation.2 | async-start | bytes 2097152 | tf_op jit(solution)/shard_map/all_to_all | solution.py:135
  78.1 30.4 %all-gather.2.cloned.1.call-done = bf16[3,2048,1024]{2,1,0:T(8,128)(2,1)} async-done(((bf16[3,128,1024]{2,1,0:T(8,128)(2,1)}), bf16[3,2048,1024]{2,1,0:T(8,128)(2,1)}) %all-gather.2.cloned.1.call-update) | async-done | bytes 12582928 | tf_op jit(solution)/shard_map/all_gather | solution.py:15
  108.5 4.4 %fusion.3 = f32[256,1024]{1,0:T(8,128)} fusion(bf16[256,2048]{1,0:T(8,128)(2,1)S(1)} %bitcast.100, bf16[3,2048,1024]{2,1,0:T(8,128)(2,1)} %all-gather.2.cloned.1.call-done), kind=kOutput, calls=%fused_computation.10 | convolution fusion | flops 1073741824 | bytes 6291456 | tf_op jit(solution)/shard_map/dot_general | solution.py:71
  112.9 4.4 %fusion.1 = f32[256,1024]{1,0:T(8,128)} fusion(bf16[256,2048]{1,0:T(8,128)(2,1)S(1)} %bitcast.101, bf16[3,2048,1024]{2,1,0:T(8,128)(2,1)} %all-gather.2.cloned.1.call-done), kind=kOutput, calls=%fused_computation.8 | convolution fusion | flops 1073741824 | bytes 6291456 | tf_op jit(solution)/shard_map/dot_general | solution.py:70
  117.3 4.4 %multiply_convert_fusion = (bf16[256,1024]{1,0:T(8,128)(2,1)S(1)}, bf16[256,1024]{1,0:T(8,128)(2,1)S(1)}, bf16[256,1024]{1,0:T(8,128)(2,1)S(1)}) fusion(f32[256,1024]{1,0:T(8,128)} %fusion.1, f32[256,1024]{1,0:T(8,128)} %fusion.3, bf16[256,2048]{1,0:T(8,128)(2,1)S(1)} %bitcast.104, bf16[3,2048,1024]{2,1,0:T(8,128)(2,1)} %all-gather.2.cloned.1.call-done), kind=kOutput, calls=%fused_computation.36 | convolution fusion | flops 1077936128 | bytes 8912896 | tf_op jit(solution)/shard_map/dot_general | solution.py:80
  121.7 1.3 convolution_convert_fusion
  123.1 1.3 convolution_convert_fusion.1
  124.4 1.3 convolution_convert_fusion.2
  125.7 21.2 %pad_maximum_fusion = bf16[2048,3072]{0,1:T(8,128)(2,1)} fusion(bf16[2048,1024]{0,1:T(8,128)(2,1)S(1)} %convolution_convert_fusion, bf16[2048,1024]{0,1:T(8,128)(2,1)S(1)} %convolution_convert_fusion.1, bf16[2048,1024]{0,1:T(8,128)(2,1)S(1)} %convolution_convert_fusion.2), kind=kLoop, calls=%fused_computation | loop fusion | flops 37748736 | bytes 25165824 | tf_op jit(solution)/shard_map/concatenate | solution.py:148
  146.9 16.6 %copy.68 = bf16[2048,3072]{1,0:T(8,128)(2,1)} copy(bf16[2048,3072]{0,1:T(8,128)(2,1)} %pad_maximum_fusion) | data formatting | bytes 25165824
  164.6 4.6 %fusion.8 = bf16[256,2048]{1,0:T(8,128)(2,1)} fusion(bf16[256,1024]{1,0:T(8,128)(2,1)S(1)} %copy-done.8, bf16[3,2048,1024]{2,1,0:T(8,128)(2,1)} %all-gather.2.cloned.1.call-done), kind=kOutput, calls=%fused_computation.17 | convolution fusion | flops 1074266112 | bytes 5767168 | tf_op jit(solution)/shard_map/dot_general | solution.py:73
  169.2 6.1 %all-to-all-start.1 = ((bf16[8,32,2048]{2,1,0:T(8,128)(2,1)}), bf16[8,32,2048]{2,1,0:T(8,128)(2,1)S(1)}, u32[]{:S(2)}, u32[]{:S(2)}) async-start(bf16[8,32,2048]{2,1,0:T(8,128)(2,1)} %bitcast.8), calls=%async_computation.1 | async-start | bytes 2097152 | tf_op jit(solution)/shard_map/all_to_all | solution.py:121
  175.3 3.5 %fusion = f32[256,2048]{1,0:T(8,128)S(1)} fusion(bf16[256,1024]{1,0:T(8,128)(2,1)S(1)} %copy-done.6, bf16[3,2048,1024]{2,1,0:T(8,128)(2,1)} %all-gather.2.cloned.1.call-done), kind=kOutput, calls=%fused_computation.7 | convolution fusion | flops 1073741824 | bytes 6815744 | tf_op jit(solution)/shard_map/dot_general | solution.py:85
  178.9 4.5 %fusion.7 = bf16[256,2048]{1,0:T(8,128)(2,1)} fusion(f32[256,2048]{1,0:T(8,128)S(1)} %fusion, bf16[256,1024]{1,0:T(8,128)(2,1)S(1)} %copy-done.4, bf16[3,2048,1024]{2,1,0:T(8,128)(2,1)} %all-gather.2.cloned.1.call-done), kind=kOutput, calls=%fused_computation.16 | convolution fusion | flops 1074790400 | bytes 7864320 | tf_op jit(solution)/shard_map/dot_general | solution.py:87
  183.4 14.9 %all-to-all-done.1 = bf16[8,32,2048]{2,1,0:T(8,128)(2,1)S(1)} async-done(((bf16[8,32,2048]{2,1,0:T(8,128)(2,1)}), bf16[8,32,2048]{2,1,0:T(8,128)(2,1)S(1)}, u32[]{:S(2)}, u32[]{:S(2)}) %all-to-all-start.1) | async-done | bytes 1048608 | tf_op jit(solution)/shard_map/all_to_all | solution.py:121
  198.3 3.6 %all-to-all-start.3 = ((bf16[8,32,2048]{2,1,0:T(8,128)(2,1)}), bf16[8,32,2048]{2,1,0:T(8,128)(2,1)S(1)}, u32[]{:S(2)}, u32[]{:S(2)}) async-start(bf16[8,32,2048]{2,1,0:T(8,128)(2,1)} %bitcast.110), calls=%async_computation.3 | async-start | bytes 2097152 | tf_op jit(solution)/shard_map/all_to_all | solution.py:141
  202.4 3.6 %fusion.18 = f32[1,128,8]{2,0,1:T(1,128)S(1)} fusion(f32[256,1,1]{0,1,2:T(1,128)S(1)} %bitcast.115, s32[128,8]{1,0:T(8,128)S(1)} %copy.59), kind=kOutput, calls=%fused_computation.42 | convolution fusion | flops 3407872 | bytes 9216 | tf_op jit(solution)/shard_map/tks,s->tk/dot_general | solution.py:128
  207.6 16.8 %all-to-all-done.3 = bf16[8,32,2048]{2,1,0:T(8,128)(2,1)S(1)} async-done(((bf16[8,32,2048]{2,1,0:T(8,128)(2,1)}), bf16[8,32,2048]{2,1,0:T(8,128)(2,1)S(1)}, u32[]{:S(2)}, u32[]{:S(2)}) %all-to-all-start.3) | async-done | bytes 1048608 | tf_op jit(solution)/shard_map/all_to_all | solution.py:141
  224.4 6.8 %all-to-all-start.4 = ((bf16[16,128,64]{1,2,0:T(8,128)(2,1)}), bf16[16,128,64]{1,2,0:T(8,128)(2,1)S(1)}, u32[]{:S(2)}, u32[]{:S(2)}) async-start(bf16[16,128,64]{1,2,0:T(8,128)(2,1)} %bitcast.98), calls=%async_computation.4 | async-start | bytes 524288 | tf_op jit(solution)/shard_map/all_to_all | solution.py:30
  231.5 1.9 fusion.14
  235.2 5.1 %all-to-all-done.4 = bf16[16,128,64]{1,2,0:T(8,128)(2,1)S(1)} async-done(((bf16[16,128,64]{1,2,0:T(8,128)(2,1)}), bf16[16,128,64]{1,2,0:T(8,128)(2,1)S(1)}, u32[]{:S(2)}, u32[]{:S(2)}) %all-to-all-start.4) | async-done | bytes 262176 | tf_op jit(solution)/shard_map/all_to_all | solution.py:30
  241.0 3.4 %all-to-all-start.5 = ((bf16[8,128,64]{1,2,0:T(8,128)(2,1)}), bf16[8,128,64]{1,2,0:T(8,128)(2,1)S(1)}, u32[]{:S(2)}, u32[]{:S(2)}) async-start(bf16[8,128,64]{1,2,0:T(8,128)(2,1)} %broadcast_in_dim.44), calls=%async_computation.5 | async-start | bytes 262144 | tf_op jit(solution)/shard_map/all_to_all | solution.py:36
  244.4 1.4 convolution_convert_fusion.5
  245.8 28.3 %psum.14 = f32[2048]{0:T(1024)S(1)} all-reduce(f32[2048]{0:T(1024)S(1)} %get-tuple-element.42), channel_id=1, replica_groups=mesh['dp'=16,'expert'=8] {'dp'}, use_global_device_ids=true, to_apply=%region_12.13 | all-reduce | flops 2048 | bytes 16384 | tf_op jit(solution)/shard_map/psum | solution.py:162
  274.1 21.5 %psum.15 = f32[2048]{0:T(1024)} all-reduce(f32[2048]{0:T(1024)S(1)} %psum.14), channel_id=1, replica_groups=mesh['dp'=16,'expert'=8] {'expert'}, use_global_device_ids=true, to_apply=%region_13.14 | all-reduce | flops 2048 | bytes 16384 | tf_op jit(solution)/shard_map/psum | solution.py:163
  (86 shorter events, 15.9 us)
Async XLA Ops:
  7.2 61.8 %copy-start = (bf16[128,2048]{1,0:T(8,128)(2,1)S(1)}, bf16[128,2048]{1,0:T(8,128)(2,1)}, u32[]{:S(2)}) copy-start(bf16[128,2048]{1,0:T(8,128)(2,1)} %param.15) | copy-start | bytes 1572868
  7.2 60.9 %copy-start.13 = (s32[128,8]{0,1:T(8,128)S(1)}, s32[128,8]{0,1:T(8,128)}, u32[]{:S(2)}) copy-start(s32[128,8]{0,1:T(8,128)} %param.11) | copy-start | bytes 12292
  7.2 60.5 %copy-start.1 = (bf16[128,2048]{1,0:T(8,128)(2,1)S(1)}, bf16[128,2048]{1,0:T(8,128)(2,1)}, u32[]{:S(2)}) copy-start(bf16[128,2048]{1,0:T(8,128)(2,1)} %param.8) | copy-start | bytes 1572868
  7.2 60.5 %copy-start.12 = (f32[2048]{0:T(1024)S(1)}, f32[2048]{0:T(1024)}, u32[]{:S(2)}) copy-start(f32[2048]{0:T(1024)} %param.9) | copy-start | bytes 24580
  7.2 18.7 %copy-start.14 = (bf16[128,64]{0,1:T(8,128)(2,1)S(1)}, bf16[128,64]{0,1:T(8,128)(2,1)}, u32[]{:S(2)}) copy-start(bf16[128,64]{0,1:T(8,128)(2,1)} %param.10) | copy-start | bytes 49156
  7.2 101.3 %all-gather.2.cloned.1.call-start = ((), (), s32[]{:S(2)}) async-start(), calls=%async_computation.7 | async-start | bytes 13369344 | tf_op jit(solution)/shard_map/all_gather | solution.py:15
  15.9 10.0 %copy-start.17 = (f32[128]{0:T(128)}, f32[128]{0:T(128)S(1)}, u32[]{:S(2)}) copy-start(f32[128]{0:T(128)S(1)} %fusion.16) | copy-start | bytes 1540
  15.9 190.3 %copy-start.15 = (f32[128]{0:T(128)}, f32[128]{0:T(128)S(1)}, u32[]{:S(2)}) copy-start(f32[128]{0:T(128)S(1)} %fusion.34) | copy-start | bytes 1540
  18.4 52.6 %all-to-all-start = ((bf16[8,32,2048]{2,1,0:T(8,128)(2,1)}), bf16[8,32,2048]{2,1,0:T(8,128)(2,1)S(1)}, u32[]{:S(2)}, u32[]{:S(2)}) async-start(bf16[8,32,2048]{2,1,0:T(8,128)(2,1)} %bitcast.3), calls=%async_computation | async-start | bytes 2097152 | tf_op jit(solution)/shard_map/all_to_all | solution.py:114
  67.0 0.7 copy-start.2
  69.0 2.1 copy-start.9
  71.1 46.3 %all-to-all-start.2 = ((bf16[8,32,2048]{2,1,0:T(8,128)(2,1)}), bf16[8,32,2048]{2,1,0:T(8,128)(2,1)S(1)}, u32[]{:S(2)}, u32[]{:S(2)}) async-start(bf16[8,32,2048]{2,1,0:T(8,128)(2,1)} %bitcast.109), calls=%async_computation.2 | async-start | bytes 2097152 | tf_op jit(solution)/shard_map/all_to_all | solution.py:135
  77.9 218.3 %reduce-scatter.4.cloned.1.call-start = ((), (), s32[]{:S(2)}) async-start(), calls=%async_computation.8 | async-start | bytes 13369344
  121.7 1.4 copy-start.7
  121.7 1.4 copy-start.3
  121.7 2.7 copy-start.5
  163.5 1.0 copy-start.8
  164.6 10.7 %copy-start.6 = (bf16[256,1024]{1,0:T(8,128)(2,1)S(1)}, bf16[256,1024]{1,0:T(8,128)(2,1)}, u32[]{:S(2)}) copy-start(bf16[256,1024]{1,0:T(8,128)(2,1)} %copy-done.5) | copy-start | bytes 1572868
  169.2 29.1 %all-to-all-start.1 = ((bf16[8,32,2048]{2,1,0:T(8,128)(2,1)}), bf16[8,32,2048]{2,1,0:T(8,128)(2,1)S(1)}, u32[]{:S(2)}, u32[]{:S(2)}) async-start(bf16[8,32,2048]{2,1,0:T(8,128)(2,1)} %bitcast.8), calls=%async_computation.1 | async-start | bytes 2097152 | tf_op jit(solution)/shard_map/all_to_all | solution.py:121
  175.3 3.5 %copy-start.4 = (bf16[256,1024]{1,0:T(8,128)(2,1)S(1)}, bf16[256,1024]{1,0:T(8,128)(2,1)}, u32[]{:S(2)}) copy-start(bf16[256,1024]{1,0:T(8,128)(2,1)} %copy-done.3) | copy-start | bytes 1572868
  198.3 26.1 %all-to-all-start.3 = ((bf16[8,32,2048]{2,1,0:T(8,128)(2,1)}), bf16[8,32,2048]{2,1,0:T(8,128)(2,1)S(1)}, u32[]{:S(2)}, u32[]{:S(2)}) async-start(bf16[8,32,2048]{2,1,0:T(8,128)(2,1)} %bitcast.110), calls=%async_computation.3 | async-start | bytes 2097152 | tf_op jit(solution)/shard_map/all_to_all | solution.py:141
  206.2 0.6 copy-start.11
  224.4 15.9 %all-to-all-start.4 = ((bf16[16,128,64]{1,2,0:T(8,128)(2,1)}), bf16[16,128,64]{1,2,0:T(8,128)(2,1)S(1)}, u32[]{:S(2)}, u32[]{:S(2)}) async-start(bf16[16,128,64]{1,2,0:T(8,128)(2,1)} %bitcast.98), calls=%async_computation.4 | async-start | bytes 524288 | tf_op jit(solution)/shard_map/all_to_all | solution.py:30
  231.2 2.9 copy-start.16
  231.5 12.9 %copy-start.10 = (f32[128,1,256]{2,1,0:T(1,128)S(1)}, f32[128,1,256]{2,1,0:T(1,128)}, u32[]{:S(2)}) copy-start(f32[128,1,256]{2,1,0:T(1,128)} %copy-done.9) | copy-start | bytes 393220
  241.0 54.6 %all-to-all-start.5 = ((bf16[8,128,64]{1,2,0:T(8,128)(2,1)}), bf16[8,128,64]{1,2,0:T(8,128)(2,1)S(1)}, u32[]{:S(2)}, u32[]{:S(2)}) async-start(bf16[8,128,64]{1,2,0:T(8,128)(2,1)} %broadcast_in_dim.44), calls=%async_computation.5 | async-start | bytes 262144 | tf_op jit(solution)/shard_map/all_to_all | solution.py:36
Sparse Core Ops, SparseCore 0:
  9.7 98.7 all-gather.1
  163.7 106.9 reduce-scatter.3
